TPU v7x, 32 devices: a 4x4x1 block of a 4x4x8 slice. The times are simulated.
32 devices in a mesh: dp: 1 (over z), tp: 4 (over y), sp: 8 (over x, core).
Axes of the slice: x: 4, y: 4, z: 1, core: 2. Of those that a mesh axis runs over, the one named last changes fastest.
The devices are a block of a 4x4x8 slice.
Arguments:
- x: bfloat16 [2048, 5120], P(('dp', 'sp'))
- pos: int32 [2048], P(('dp', 'sp'))
- k_hist: bfloat16 [2, 8192, 8, 128], P(None, ('dp', 'sp'), 'tp')
- v_hist: bfloat16 [2, 8192, 8, 128], P(None, ('dp', 'sp'), 'tp')
- wq: bfloat16 [2, 5120, 5120], P(None, None, 'tp')
- wk: bfloat16 [2, 5120, 1024], P(None, None, 'tp')
- wv: bfloat16 [2, 5120, 1024], P(None, None, 'tp')
- wo: bfloat16 [2, 5120, 5120], P(None, 'tp')
- wg: bfloat16 [2, 5120, 13824], P(None, None, 'tp')
- wu: bfloat16 [2, 5120, 13824], P(None, None, 'tp')
- wd: bfloat16 [2, 13824, 5120], P(None, 'tp')
- g1: bfloat16 [2, 5120], replicated
- g2: bfloat16 [2, 5120], replicated
Outputs:
- output 1: bfloat16 [2048, 5120], P(('dp', 'sp'))
- output 2: bfloat16 [2, 2048, 8, 128], P(None, ('dp', 'sp'), 'tp')
- output 3: bfloat16 [2, 2048, 8, 128], P(None, ('dp', 'sp'), 'tp')
All inputs are finite; a program needn't handle non-finite values.
Results may differ from a plain program's by a relative error of at most 0.02.
Values are sent between devices in bfloat16 or wider.
A program may use at most 768 MiB of HBM per device.

v0:
```python
import jax
import jax.numpy as jnp
from jax import lax
from jax.sharding import PartitionSpec as P

EPS = 1e-5
ROPE_THETA = 500000.0
QB = 64


def rmsnorm(x, g):
    xf = x.astype(jnp.float32)
    r = lax.rsqrt(jnp.mean(xf * xf, axis=-1, keepdims=True) + EPS)
    return (xf * r * g.astype(jnp.float32)).astype(jnp.bfloat16)


def rope(t, pos):
    half = t.shape[-1] // 2
    inv = ROPE_THETA ** (-(jnp.arange(half, dtype=jnp.float32) * (2.0 / t.shape[-1])))
    ang = pos.astype(jnp.float32)[..., None] * inv
    c = jnp.cos(ang)[..., None, :]
    s = jnp.sin(ang)[..., None, :]
    tf = t.astype(jnp.float32)
    t1 = tf[..., :half]
    t2 = tf[..., half:]
    return jnp.concatenate([t1 * c - t2 * s, t2 * c + t1 * s], axis=-1).astype(jnp.bfloat16)


def mm(a, b):
    return jnp.dot(a, b, preferred_element_type=jnp.float32)


def partial_attn(qq, k, v, mask=None):
    s = jnp.einsum('qkgd,tkd->qkgt', qq, k, preferred_element_type=jnp.float32) * (k.shape[-1] ** -0.5)
    if mask is not None:
        s = jnp.where(mask, s, -jnp.inf)
    m = jnp.max(s, axis=-1)
    p = jnp.exp(s - m[..., None])
    o = jnp.einsum('qkgt,tkd->qkgd', p.astype(jnp.bfloat16), v, preferred_element_type=jnp.float32)
    return m, jnp.sum(p, axis=-1), o


def solution(mesh):
    sp = mesh.shape['sp']
    row = ('dp', 'sp')
    kv_spec = P(None, row, 'tp', None)
    col = P(None, None, 'tp')
    rowsplit = P(None, 'tp', None)

    def body(x, pos, k_hist, v_hist, wq, wk, wv, wo, wg, wu, wd, g1, g2):
        n, d = x.shape
        layers, _, kvl, dh = k_hist.shape
        hql = wq.shape[-1] // dh
        g = hql // kvl
        s_tot = n * sp
        idx = lax.axis_index('sp')
        kpos = jnp.arange(s_tot)
        starts = idx * n + jnp.arange(n // QB) * QB
        ks, vs = [], []
        for l in range(layers):
            h = rmsnorm(x, g1[l])
            q = rope(mm(h, wq[l]).astype(jnp.bfloat16).reshape(n, hql, dh), pos)
            k = rope(mm(h, wk[l]).astype(jnp.bfloat16).reshape(n, kvl, dh), pos)
            v = mm(h, wv[l]).astype(jnp.bfloat16).reshape(n, kvl, dh)
            ks.append(k)
            vs.append(v)

            q_all = lax.all_gather(q, 'sp', axis=0, tiled=True).reshape(s_tot // QB, QB, kvl, g, dh)
            kh = k_hist[l]
            vh = v_hist[l]
            m_h, l_h, o_h = lax.map(lambda qq: partial_attn(qq, kh, vh), q_all)
            m_h = m_h.reshape(s_tot, kvl, g)
            m_g = lax.pmax(m_h, 'sp')
            sc = jnp.exp(m_h - m_g)
            o_h = lax.psum_scatter(o_h.reshape(s_tot, kvl, g, dh) * sc[..., None], 'sp', scatter_dimension=0, tiled=True)
            l_h = lax.psum_scatter(l_h.reshape(s_tot, kvl, g) * sc, 'sp', scatter_dimension=0, tiled=True)
            m_h = lax.dynamic_slice_in_dim(m_g, idx * n, n, axis=0)

            k_all = lax.all_gather(k, 'sp', axis=0, tiled=True)
            v_all = lax.all_gather(v, 'sp', axis=0, tiled=True)

            def new_blk(args, k_all=k_all, v_all=v_all):
                st, qq = args
                mask = (kpos[None, :] <= (st + jnp.arange(QB))[:, None])[:, None, None, :]
                return partial_attn(qq, k_all, v_all, mask)

            m_n, l_n, o_n = lax.map(new_blk, (starts, q.reshape(n // QB, QB, kvl, g, dh)))
            m_n = m_n.reshape(n, kvl, g)
            l_n = l_n.reshape(n, kvl, g)
            o_n = o_n.reshape(n, kvl, g, dh)
            mt = jnp.maximum(m_h, m_n)
            a_h = jnp.exp(m_h - mt)
            a_n = jnp.exp(m_n - mt)
            den = l_h * a_h + l_n * a_n
            o = (o_h * a_h[..., None] + o_n * a_n[..., None]) / den[..., None]
            attn = o.astype(jnp.bfloat16).reshape(n, hql * dh)
            x = x + lax.psum(mm(attn, wo[l]), 'tp').astype(jnp.bfloat16)

            h2 = rmsnorm(x, g2[l])
            a = mm(h2, wg[l]).astype(jnp.bfloat16)
            b = mm(h2, wu[l]).astype(jnp.bfloat16)
            u = (jax.nn.silu(a.astype(jnp.float32)) * b.astype(jnp.float32)).astype(jnp.bfloat16)
            x = x + lax.psum(mm(u, wd[l]), 'tp').astype(jnp.bfloat16)
        return x, jnp.stack(ks), jnp.stack(vs)

    in_specs = (P(row, None), P(row), kv_spec, kv_spec, col, col, col, rowsplit, col, col, rowsplit, P(), P())
    out_specs = (P(row, None), kv_spec, kv_spec)
    return jax.shard_map(body, mesh=mesh, in_specs=in_specs, out_specs=out_specs, check_vma=False)
```

profile of v0, /device:TPU:100, one launch (start us, length us, event | category | flops | bytes accessed | tf_op | source)
XLA Modules:
  0.0 1295.2 jit_solution(13964077225910324634)
XLA Ops:
  11.1 10.2 fusion.189
  21.3 3.0 copy.84
  28.2 3.2 fusion.206
  32.1 2.8 fusion.242
  36.6 29.8 %all-gather.7.cloned.1.call-done = bf16[2048,10,128]{0,2,1:T(8,128)(2,1)} async-done(((bf16[256,10,128]{0,2,1:T(8,128)(2,1)}), bf16[2048,10,128]{0,2,1:T(8,128)(2,1)}) %all-gather.7.cloned.1.call-update) | async-done | bytes 5242896 | tf_op jit(solution)/shard_map/all_gather | solution.py:68
  66.4 7.8 copy.85
  74.2 5.2 broadcast.187.clone2
  79.4 116.7 %while.58 = (s32[]{:T(128)}, f32[32,64,2,5]{1,0,2,3:T(8,128)S(1)}, f32[32,64,2,5]{1,0,2,3:T(8,128)S(1)}, f32[32,64,2,5,128]{4,1,0,3,2:T(8,128)}, bf16[32,64,2,5,...) while((s32[]{:T(128)}, f32[32,64,2,5]{1,0,2,3:T(8,128)S(1)}, ...), condition=%wide.region_4.5_spmd, body=%wide.region_1.4_spmd.sunk | while | flops 340785920 | bytes 9436261 | solution.py:71
  198.6 3.9 fusion.209
  203.5 44.3 %all-reduce.7.cloned.1.call-done = f32[2048,2,5]{0,1,2:T(2,128)} async-done(((f32[2048,2,5]{0,1,2:T(2,128)}), f32[2048,2,5]{0,1,2:T(2,128)}) %all-reduce.7.cloned.1.call-update) | async-done | bytes 81936 | tf_op jit(solution)/shard_map/pmax | solution.py:73
  248.8 4.8 copy.138
  253.5 6.1 reshape.327
  259.8 11.0 bitcast_multiply_fusion.1
  276.2 19.6 %all-gather.11.cloned.1.call-done = bf16[2048,2,128]{2,0,1:T(8,128)(2,1)} async-done(((bf16[256,2,128]{2,0,1:T(8,128)(2,1)}), bf16[2048,2,128]{2,0,1:T(8,128)(2,1)}) %all-gather.11.cloned.1.call-update) | async-done | bytes 1048592 | tf_op jit(solution)/shard_map/all_gather | solution.py:80
  296.0 20.3 %while.60 = (s32[]{:T(128)}, f32[4,64,2,5]{1,0,2,3:T(4,128)S(1)}, f32[4,64,2,5]{1,0,2,3:T(4,128)S(1)}, f32[4,64,2,5,128]{4,1,0,3,2:T(8,128)S(1)}, s32[4]{0:T(128...) while((s32[]{:T(128)}, f32[4,64,2,5]{1,0,2,3:T(4,128)S(1)}, ...), condition=%wide.region_10.11_spmd.clone, body=%wide.region_7.10_spmd.clone.sunk | while | flops 685636416 | bytes 23072928 | solution.py:87
  316.4 8.0 reduce-scatter.13.cloned.1.call-done
  326.6 61.6 %reduce-scatter.9.cloned.1.call-done = f32[256,2,5,128]{3,0,2,1:T(8,128)} async-done(((f32[2048,2,5,128]{3,0,2,1:T(8,128)}), f32[256,2,5,128]{3,0,2,1:T(8,128)}) %reduce-scatter.9.cloned.1.call-update) | async-done | bytes 1310736 | tf_op jit(solution)/shard_map/reduce_scatter | solution.py:75
  390.8 10.7 fusion.106
  401.4 99.2 %all-reduce.10 = bf16[256,5120]{1,0:T(8,128)(2,1)} all-reduce(f32[256,5120]{1,0:T(8,128)} %fusion.106), channel_id=1, replica_groups=mesh['dp'=1,'tp'=4,'sp'=8] {'tp'}, use_global_device_ids=true, to_apply=%region_12.13 | all-reduce | flops 1310720 | bytes 7864320 | tf_op jit(solution)/shard_map/psum | solution.py:97
  500.6 2.9 fusion.117
  503.6 17.0 %fusion.129 = f32[256,3456]{1,0:T(8,128)S(1)} fusion(bf16[2,5120,3456]{2,1,0:T(8,128)(2,1)} %param.29, bf16[256,5120]{1,0:T(8,128)(2,1)S(1)} %get-tuple-element.387, f32[5120]{0:T(1024)S(1)} %bitcast.474, f32[256]{0:T(256)S(1)} %add_rsqrt_fusion.2), kind=kOutput, calls=%fused_computation.129 | convolution fusion | flops 9066708992 | bytes 41571328 | tf_op jit(solution)/shard_map/dot_general | solution.py:30
  520.6 16.3 %fusion.141.clone.5 = bf16[256,3456]{1,0:T(8,128)(2,1)S(1)} fusion(bf16[2,5120,3456]{2,1,0:T(8,128)(2,1)} %param.30, f32[256,3456]{1,0:T(8,128)S(1)} %fusion.129, bf16[256,5120]{1,0:T(8,128)(2,1)S(1)} %get-tuple-element.387, f32[5120]{0:T(1024)S(1)} %bitcast.475, f32[256]{0:T(256)S(1)} %add_rsqrt_fusion.2), kind=kOutput, calls=%fused_computation.133.clone.clone.clone.2 | convolution fusion | flops 9072017408 | bytes 43340800 | tf_op jit(solution)/shard_map/dot_general | solution.py:30
  537.0 17.5 %fusion.90 = f32[256,5120]{1,0:T(8,128)} fusion(bf16[2,3456,5120]{2,1,0:T(8,128)(2,1)} %param.31, bf16[256,3456]{1,0:T(8,128)(2,1)S(1)} %fusion.141.clone.5), kind=kOutput, calls=%fused_computation.82 | convolution fusion | flops 9059696640 | bytes 42401792 | tf_op jit(solution)/shard_map/dot_general | solution.py:30
  554.5 94.6 %all-reduce.11 = bf16[256,5120]{1,0:T(8,128)(2,1)} all-reduce(f32[256,5120]{1,0:T(8,128)} %fusion.90), channel_id=1, replica_groups=mesh['dp'=1,'tp'=4,'sp'=8] {'tp'}, use_global_device_ids=true, to_apply=%region_14.15 | all-reduce | flops 1310720 | bytes 7864320 | tf_op jit(solution)/shard_map/psum | solution.py:103
  649.1 3.0 fusion.120
  653.6 9.5 fusion.195
  666.3 4.0 fusion.212
  671.0 32.3 %all-gather.13.cloned.1.call-done = bf16[2048,10,128]{0,2,1:T(8,128)(2,1)} async-done(((bf16[256,10,128]{0,2,1:T(8,128)(2,1)}), bf16[2048,10,128]{0,2,1:T(8,128)(2,1)}) %all-gather.13.cloned.1.call-update) | async-done | bytes 5242896 | tf_op jit(solution)/shard_map/all_gather | solution.py:68
  703.2 7.8 copy.108
  711.0 5.2 broadcast.187.clone
  716.2 116.7 %while.59 = (s32[]{:T(128)}, f32[32,64,2,5]{1,0,2,3:T(8,128)S(1)}, f32[32,64,2,5]{1,0,2,3:T(8,128)S(1)}, f32[32,64,2,5,128]{4,1,0,3,2:T(8,128)}, bf16[32,64,2,5,...) while((s32[]{:T(128)}, f32[32,64,2,5]{1,0,2,3:T(8,128)S(1)}, ...), condition=%wide.region_19.20_spmd, body=%wide.region_16.19_spmd.sunk | while | flops 340785920 | bytes 9436261 | solution.py:71
  835.1 3.9 fusion.215
  840.1 44.5 %all-reduce.9.cloned.1.call-done = f32[2048,2,5]{0,1,2:T(2,128)} async-done(((f32[2048,2,5]{0,1,2:T(2,128)}), f32[2048,2,5]{0,1,2:T(2,128)}) %all-reduce.9.cloned.1.call-update) | async-done | bytes 81936 | tf_op jit(solution)/shard_map/pmax | solution.py:73
  885.5 4.8 copy.140
  890.3 6.1 reshape.329
  896.6 11.0 bitcast_multiply_fusion
  917.4 14.0 %all-gather.17.cloned.1.call-done = bf16[2048,2,128]{2,0,1:T(8,128)(2,1)} async-done(((bf16[256,2,128]{2,0,1:T(8,128)(2,1)}), bf16[2048,2,128]{2,0,1:T(8,128)(2,1)}) %all-gather.17.cloned.1.call-update) | async-done | bytes 1048592 | tf_op jit(solution)/shard_map/all_gather | solution.py:80
  931.6 19.9 %while.61 = (s32[]{:T(128)}, f32[4,64,2,5]{1,0,2,3:T(4,128)S(1)}, f32[4,64,2,5]{1,0,2,3:T(4,128)S(1)}, f32[4,64,2,5,128]{4,1,0,3,2:T(8,128)S(1)}, s32[4]{0:T(128...) while((s32[]{:T(128)}, f32[4,64,2,5]{1,0,2,3:T(4,128)S(1)}, ...), condition=%wide.region_25.26_spmd.clone, body=%wide.region_22.25_spmd.clone.sunk | while | flops 685636416 | bytes 23072928 | solution.py:87
  951.7 8.0 reduce-scatter.15.cloned.1.call-done
  961.9 61.6 %reduce-scatter.11.cloned.1.call-done = f32[256,2,5,128]{3,0,2,1:T(8,128)} async-done(((f32[2048,2,5,128]{3,0,2,1:T(8,128)}), f32[256,2,5,128]{3,0,2,1:T(8,128)}) %reduce-scatter.11.cloned.1.call-update) | async-done | bytes 1310736 | tf_op jit(solution)/shard_map/reduce_scatter | solution.py:75
  1026.0 10.7 fusion.102
  1036.7 99.2 %all-reduce.12 = bf16[256,5120]{1,0:T(8,128)(2,1)} all-reduce(f32[256,5120]{1,0:T(8,128)} %fusion.102), channel_id=1, replica_groups=mesh['dp'=1,'tp'=4,'sp'=8] {'tp'}, use_global_device_ids=true, to_apply=%region_27.28 | all-reduce | flops 1310720 | bytes 7864320 | tf_op jit(solution)/shard_map/psum | solution.py:97
  1135.8 3.0 fusion.123
  1138.8 17.1 %fusion.147 = f32[256,3456]{1,0:T(8,128)S(1)} fusion(bf16[2,5120,3456]{2,1,0:T(8,128)(2,1)} %param.29, bf16[256,5120]{1,0:T(8,128)(2,1)S(1)} %get-tuple-element.378, f32[5120]{0:T(1024)S(1)} %bitcast.469, f32[256]{0:T(256)S(1)} %add_rsqrt_fusion), kind=kOutput, calls=%fused_computation.135 | convolution fusion | flops 9066708992 | bytes 41571328 | tf_op jit(solution)/shard_map/dot_general | solution.py:30
  1156.0 16.1 %fusion.159.clone.5 = bf16[256,3456]{1,0:T(8,128)(2,1)S(1)} fusion(bf16[2,5120,3456]{2,1,0:T(8,128)(2,1)} %param.30, f32[256,3456]{1,0:T(8,128)S(1)} %fusion.147, bf16[256,5120]{1,0:T(8,128)(2,1)S(1)} %get-tuple-element.378, f32[5120]{0:T(1024)S(1)} %bitcast.470, f32[256]{0:T(256)S(1)} %add_rsqrt_fusion), kind=kOutput, calls=%fused_computation.139.clone.clone.clone.2 | convolution fusion | flops 9072017408 | bytes 43340800 | tf_op jit(solution)/shard_map/dot_general | solution.py:30
  1172.1 17.5 %fusion.84 = f32[256,5120]{1,0:T(8,128)} fusion(bf16[2,3456,5120]{2,1,0:T(8,128)(2,1)} %param.31, bf16[256,3456]{1,0:T(8,128)(2,1)S(1)} %fusion.159.clone.5), kind=kOutput, calls=%fused_computation.76 | convolution fusion | flops 9059696640 | bytes 42401792 | tf_op jit(solution)/shard_map/dot_general | solution.py:30
  1189.6 94.2 %all-reduce.13 = bf16[256,5120]{1,0:T(8,128)(2,1)} all-reduce(f32[256,5120]{1,0:T(8,128)} %fusion.84), channel_id=1, replica_groups=mesh['dp'=1,'tp'=4,'sp'=8] {'tp'}, use_global_device_ids=true, to_apply=%region_29.30 | all-reduce | flops 1310720 | bytes 7864320 | tf_op jit(solution)/shard_map/psum | solution.py:103
  1283.8 4.2 add.198
  (737 shorter events, 318.6 us)
Async XLA Ops:
  7.2 59.2 %all-gather.7.cloned.1.call-start = ((), (), s32[]{:S(2)}) async-start(), calls=%async_computation.4 | async-start | bytes 5898240 | tf_op jit(solution)/shard_map/all_gather | solution.py:68
  11.1 13.2 %copy-start.38 = (s32[256]{0:T(256)S(1)}, s32[256]{0:T(256)}, u32[]{:S(2)}) copy-start(s32[256]{0:T(256)} %param.22) | copy-start | bytes 3076
  21.3 7.0 copy-start
  27.0 220.7 %all-reduce.7.cloned.1.call-start = ((), (), s32[]{:S(2)}) async-start(), calls=%async_computation.5 | async-start | bytes 163840 | tf_op jit(solution)/shard_map/pmax | solution.py:73
  27.2 4.6 copy-start.18
  28.2 3.6 copy-start.20
  31.4 3.5 copy-start.26
  32.1 164.9 %copy-start.10 = (bf16[256,2,64]{2,1,0:T(2,128)(2,1)}, bf16[256,2,64]{2,1,0:T(2,128)(2,1)S(1)}, u32[]{:S(2)}) copy-start(bf16[256,2,64]{2,1,0:T(2,128)(2,1)S(1)} %get-tuple-element.411) | copy-start | bytes 196612
  32.1 164.9 %copy-start.12 = (bf16[256,2,64]{2,1,0:T(2,128)(2,1)}, bf16[256,2,64]{2,1,0:T(2,128)(2,1)S(1)}, u32[]{:S(2)}) copy-start(bf16[256,2,64]{2,1,0:T(2,128)(2,1)S(1)} %get-tuple-element.412) | copy-start | bytes 196612
  79.4 119.1 %copy-start.37 = (f32[1,5120]{1,0:T(1,128)S(1)}, f32[1,5120]{1,0:T(1,128)}, u32[]{:S(2)}) copy-start(f32[1,5120]{1,0:T(1,128)} %copy-done.36) | copy-start | bytes 61444
  196.9 77.9 %all-gather.9.cloned.1.call-start = ((), (), s32[]{:S(2)}) async-start(), calls=%async_computation.7 | async-start | bytes 1179648 | tf_op jit(solution)/shard_map/all_gather | solution.py:79
  198.1 49.7 %copy-start.27 = (f32[2048,2,5]{0,1,2:T(2,128)S(1)}, f32[2048,2,5]{0,1,2:T(2,128)}, u32[]{:S(2)}) copy-start(f32[2048,2,5]{0,1,2:T(2,128)} %reshape.295) | copy-start | bytes 245764
  198.1 97.7 %all-gather.11.cloned.1.call-start = ((), (), s32[]{:S(2)}) async-start(), calls=%async_computation.8 | async-start | bytes 1179648 | tf_op jit(solution)/shard_map/all_gather | solution.py:80
  202.5 51.0 %copy-start.29 = (bf16[256,256]{0,1:T(8,128)(2,1)}, bf16[256,256]{0,1:T(8,128)(2,1)S(1)}, u32[]{:S(2)}) copy-start(bf16[256,256]{0,1:T(8,128)(2,1)S(1)} %fusion.209) | copy-start | bytes 393220
  203.3 121.1 %reduce-scatter.13.cloned.1.call-start = ((), (), s32[]{:S(2)}) async-start(), calls=%async_computation.14 | async-start | bytes 1179648
  259.7 128.5 %reduce-scatter.9.cloned.1.call-start = ((), (), s32[]{:S(2)}) async-start(), calls=%async_computation.6 | async-start | bytes 11796480 | tf_op jit(solution)/shard_map/reduce_scatter | solution.py:75
  270.9 3.3 copy-start.33
  270.9 432.3 %all-gather.13.cloned.1.call-start = ((), (), s32[]{:S(2)}) async-start(), calls=%async_computation.9 | async-start | bytes 5898240 | tf_op jit(solution)/shard_map/all_gather | solution.py:68
  316.3 74.5 %copy-start.41 = (s32[4]{0:T(128)}, s32[4]{0:T(128)S(1)}, u32[]{:S(2)}) copy-start(s32[4]{0:T(128)S(1)} %get-tuple-element.789) | copy-start | bytes 52
  401.4 99.2 %copy-start.1 = (bf16[256,5120]{1,0:T(8,128)(2,1)S(1)}, bf16[256,5120]{1,0:T(8,128)(2,1)}, u32[]{:S(2)}) copy-start(bf16[256,5120]{1,0:T(8,128)(2,1)} %param.21) | copy-start | bytes 7864324
  503.5 17.1 %copy-start.4 = (bf16[256,5120]{1,0:T(8,128)(2,1)}, bf16[256,5120]{1,0:T(8,128)(2,1)S(1)}, u32[]{:S(2)}) copy-start(bf16[256,5120]{1,0:T(8,128)(2,1)S(1)} %get-tuple-element.387) | copy-start | bytes 7864324
  554.5 94.6 %copy-start.5 = (bf16[256,5120]{1,0:T(8,128)(2,1)S(1)}, bf16[256,5120]{1,0:T(8,128)(2,1)}, u32[]{:S(2)}) copy-start(bf16[256,5120]{1,0:T(8,128)(2,1)} %copy-done.4) | copy-start | bytes 7864324
  649.1 4.5 copy-start.34
  653.6 11.3 copy-start.23
  653.6 11.3 copy-start.25
  663.1 3.1 copy-start.8
  663.1 3.1 copy-start.9
  666.1 218.5 %all-reduce.9.cloned.1.call-start = ((), (), s32[]{:S(2)}) async-start(), calls=%async_computation.10 | async-start | bytes 163840 | tf_op jit(solution)/shard_map/pmax | solution.py:73
  666.3 4.3 copy-start.19
  666.3 4.3 copy-start.21
  670.9 162.9 %copy-start.14 = (bf16[256,2,64]{2,1,0:T(2,128)(2,1)}, bf16[256,2,64]{2,1,0:T(2,128)(2,1)S(1)}, u32[]{:S(2)}) copy-start(bf16[256,2,64]{2,1,0:T(2,128)(2,1)S(1)} %get-tuple-element.409) | copy-start | bytes 196612
  670.9 162.9 %copy-start.16 = (bf16[256,2,64]{2,1,0:T(2,128)(2,1)}, bf16[256,2,64]{2,1,0:T(2,128)(2,1)S(1)}, u32[]{:S(2)}) copy-start(bf16[256,2,64]{2,1,0:T(2,128)(2,1)S(1)} %get-tuple-element.410) | copy-start | bytes 196612
  833.7 82.4 %all-gather.15.cloned.1.call-start = ((), (), s32[]{:S(2)}) async-start(), calls=%async_computation.12 | async-start | bytes 1179648 | tf_op jit(solution)/shard_map/all_gather | solution.py:79
  834.9 49.7 %copy-start.28 = (f32[2048,2,5]{0,1,2:T(2,128)S(1)}, f32[2048,2,5]{0,1,2:T(2,128)}, u32[]{:S(2)}) copy-start(f32[2048,2,5]{0,1,2:T(2,128)} %reshape.304) | copy-start | bytes 245764
  834.9 96.5 %all-gather.17.cloned.1.call-start = ((), (), s32[]{:S(2)}) async-start(), calls=%async_computation.13 | async-start | bytes 1179648 | tf_op jit(solution)/shard_map/all_gather | solution.py:80
  839.1 51.2 %copy-start.31 = (bf16[256,256]{0,1:T(8,128)(2,1)}, bf16[256,256]{0,1:T(8,128)(2,1)S(1)}, u32[]{:S(2)}) copy-start(bf16[256,256]{0,1:T(8,128)(2,1)S(1)} %fusion.215) | copy-start | bytes 393220
  839.9 119.8 %reduce-scatter.15.cloned.1.call-start = ((), (), s32[]{:S(2)}) async-start(), calls=%async_computation.15 | async-start | bytes 1179648
  896.5 126.9 %reduce-scatter.11.cloned.1.call-start = ((), (), s32[]{:S(2)}) async-start(), calls=%async_computation.11 | async-start | bytes 11796480 | tf_op jit(solution)/shard_map/reduce_scatter | solution.py:75
  909.3 5.4 copy-start.11
  909.3 5.4 copy-start.13
  909.6 5.1 copy-start.15
  909.6 5.1 copy-start.17
  909.9 3.7 copy-start.32
  910.9 20.7 %copy-start.42 = (s32[4]{0:T(128)S(1)}, s32[4]{0:T(128)}, u32[]{:S(2)}) copy-start(s32[4]{0:T(128)} %copy-done.41) | copy-start | bytes 52
  1036.6 99.2 %copy-start.3 = (bf16[256,5120]{1,0:T(8,128)(2,1)S(1)}, bf16[256,5120]{1,0:T(8,128)(2,1)}, u32[]{:S(2)}) copy-start(bf16[256,5120]{1,0:T(8,128)(2,1)} %copy-done.2) | copy-start | bytes 7864324
  1135.8 3.0 copy-start.35
  1138.8 17.2 %copy-start.6 = (bf16[256,5120]{1,0:T(8,128)(2,1)}, bf16[256,5120]{1,0:T(8,128)(2,1)S(1)}, u32[]{:S(2)}) copy-start(bf16[256,5120]{1,0:T(8,128)(2,1)S(1)} %get-tuple-element.378) | copy-start | bytes 7864324
  1189.6 94.2 %copy-start.7 = (bf16[256,5120]{1,0:T(8,128)(2,1)S(1)}, bf16[256,5120]{1,0:T(8,128)(2,1)}, u32[]{:S(2)}) copy-start(bf16[256,5120]{1,0:T(8,128)(2,1)} %copy-done.6) | copy-start | bytes 7864324
  (13 other events, 28.9 us)
Sparse Core Ops, SparseCore 0:
  27.2 39.2 all-gather.6
  197.1 50.6 all-reduce.6
  250.0 23.3 all-gather.8
  275.4 20.3 all-gather.10
  298.5 25.9 reduce-scatter.12
  326.6 61.5 reduce-scatter.8
  666.2 36.9 all-gather.12
  833.8 50.6 all-reduce.8
  886.2 23.3 all-gather.14
  911.0 20.3 all-gather.16
  933.7 25.9 reduce-scatter.14
  961.9 61.5 reduce-scatter.10
where the time goes:
time: 1310 us; the launch traced here: 1300 us
  blocking collectives  387 us (30%)
  matrix products  359 us (27%)
  waiting for transfers between devices  324 us (25%)
  other arithmetic  115 us (9%)
  local copies, waits for them, and re-layouts  89.6 us (7%)
  between operations  15.6 us (1%)
    psum x2, blocking collectives, body(): x = x + lax.psum(mm(attn, wo[l]), 'tp').astype(jnp.bfloat16)  198 us
    psum x2, blocking collectives, body(): x = x + lax.psum(mm(u, wd[l]), 'tp').astype(jnp.bfloat16)  189 us
    dot_general x14, matrix products, mm(): return jnp.dot(a, b, preferred_element_type=jnp.float32)  158 us
    reduce_scatter x2, waiting for transfers between devices, body(): lax.psum_scatter(o_h.reshape(s_tot, kvl, g, dh) * sc[..., None], 'sp', sc...  123 us
    dot_general x72, matrix products, partial_attn(): jnp.einsum('qkgd,tkd->qkgt', qq, k, preferred_element_type=jnp.float32)  104 us
    dot_general x72, matrix products, partial_attn(): jnp.einsum('qkgt,tkd->qkgd', p.astype(jnp.bfloat16), v, preferred_element...  96.7 us
    pmax x2, waiting for transfers between devices, body(): m_g = lax.pmax(m_h, 'sp')  88.7 us
    all_gather x2, waiting for transfers between devices, body(): lax.all_gather(q, 'sp', axis=0, tiled=True)  62.1 us
  transfers between devices with their start and end apart: 12, of which 10 were waited for; matrix products, arithmetic and copies ran while one was open for 10% of the time, Pallas kernels for 0%

commit v1 on v0

v1 whole, which is shorter than its diff:
```python
import functools

import jax
import jax.numpy as jnp
from jax import lax
from jax.experimental import pallas as pl
from jax.experimental.pallas import tpu as pltpu
from jax.sharding import PartitionSpec as P

EPS = 1e-5
ROPE_THETA = 500000.0
LOG2E = 1.4426950408889634
CHUNK = 1024
PARAMS2 = pltpu.CompilerParams(
    dimension_semantics=('arbitrary', 'arbitrary'), vmem_limit_bytes=48 * 1024 * 1024)
PARAMS1 = pltpu.CompilerParams(dimension_semantics=('arbitrary',), vmem_limit_bytes=48 * 1024 * 1024)


def rmsnorm(x, g):
    xf = x.astype(jnp.float32)
    r = lax.rsqrt(jnp.mean(xf * xf, axis=-1, keepdims=True) + EPS)
    return (xf * r * g.astype(jnp.float32)).astype(jnp.bfloat16)


def mm(a, b):
    return jnp.dot(a, b, preferred_element_type=jnp.float32)


def rope_tables(pos, dh):
    half = dh // 2
    inv = ROPE_THETA ** (-(jnp.arange(half, dtype=jnp.float32) * (2.0 / dh)))
    ang = pos.astype(jnp.float32)[:, None] * inv
    c = jnp.cos(ang)
    s = jnp.sin(ang)
    return jnp.concatenate([c, c], axis=-1), jnp.concatenate([-s, s], axis=-1)


def qkv_kernel(nq, h_ref, wq_ref, wk_ref, wv_ref, c_ref, s_ref, q_ref, k_ref, v_ref):
    j = pl.program_id(0)
    dh = c_ref.shape[-1]

    def turn(w_ref, out_ref):
        t = mm(h_ref[...], w_ref[...]).astype(jnp.bfloat16).astype(jnp.float32)
        for i in range(t.shape[-1] // dh):
            th = t[:, i * dh:(i + 1) * dh]
            r = th * c_ref[...] + pltpu.roll(th, dh // 2, 1) * s_ref[...]
            out_ref[:, i * dh:(i + 1) * dh] = r.astype(out_ref.dtype)

    @pl.when(j < nq)
    def _():
        turn(wq_ref, q_ref)

    @pl.when(j == nq)
    def _():
        turn(wk_ref, k_ref)

    @pl.when(j == nq + 1)
    def _():
        v_ref[...] = mm(h_ref[...], wv_ref[...]).astype(v_ref.dtype)


def qkv(h, wq, wk, wv, l, c, s):
    n, d = h.shape
    kvw = wk.shape[-1]
    nq = wq.shape[-1] // kvw
    full = lambda r, w: pl.BlockSpec((r, w), lambda j: (0, 0))
    weight = lambda at: pl.BlockSpec((None, d, kvw), lambda j: (l, 0, at(j)))
    first = lambda j: jnp.minimum(j, nq - 1)
    zero = lambda j: 0
    out = lambda w: jax.ShapeDtypeStruct((n, w), jnp.bfloat16)
    return pl.pallas_call(
        functools.partial(qkv_kernel, nq),
        grid=(nq + 2,),
        in_specs=[full(n, d), weight(first), weight(zero), weight(zero), full(*c.shape), full(*s.shape)],
        out_specs=[pl.BlockSpec((n, kvw), lambda j: (0, first(j))), full(n, kvw), full(n, kvw)],
        out_shape=(out(wq.shape[-1]), out(kvw), out(kvw)),
        compiler_params=PARAMS1,
        cost_estimate=pl.CostEstimate(
            flops=2 * n * d * (nq + 2) * kvw, bytes_accessed=2 * d * (nq + 2) * kvw, transcendentals=0),
        name='qkv',
    )(h, wq, wk, wv, c, s)


def gate_kernel(h_ref, wg_ref, wu_ref, u_ref):
    a = mm(h_ref[...], wg_ref[...]).astype(jnp.bfloat16).astype(jnp.float32)
    b = mm(h_ref[...], wu_ref[...]).astype(jnp.bfloat16).astype(jnp.float32)
    u_ref[...] = (jax.nn.silu(a) * b).astype(u_ref.dtype)


def down_kernel(u_ref, w_ref, o_ref):
    o_ref[...] = mm(u_ref[...], w_ref[...])


def by_columns(kernel, x, ws, l, cols, dtype, name):
    n, d = x.shape
    f = ws[0].shape[-1]
    cols = min(cols, f)
    return pl.pallas_call(
        kernel,
        grid=(pl.cdiv(f, cols),),
        in_specs=[pl.BlockSpec((n, d), lambda j: (0, 0))] + [pl.BlockSpec((None, d, cols), lambda j: (l, 0, j))] * len(ws),
        out_specs=pl.BlockSpec((n, cols), lambda j: (0, j)),
        out_shape=jax.ShapeDtypeStruct((n, f), dtype),
        compiler_params=PARAMS1,
        cost_estimate=pl.CostEstimate(
            flops=2 * len(ws) * n * d * f, bytes_accessed=2 * len(ws) * d * f, transcendentals=0),
        name=name,
    )(x, *ws)


def block(q, k, v, m, l, acc, scale, mask=None):
    s = lax.dot_general(q, k, (((1,), (1,)), ((), ())), preferred_element_type=jnp.float32)
    if mask is not None:
        s = jnp.where(mask, s, -jnp.inf)
    top = jnp.max(s, axis=-1, keepdims=True)
    m_new = top if m is None else jnp.maximum(m, top)
    p = jnp.exp2((s - m_new) * (scale * LOG2E))
    width = v.shape[-1]
    part = p[:, :width]
    for j in range(1, p.shape[-1] // width):
        part = part + p[:, j * width:(j + 1) * width]
    o = lax.dot_general(p.astype(jnp.bfloat16), v, (((1,), (0,)), ((), ())), preferred_element_type=jnp.float32)
    if m is None:
        return m_new, part, o
    a = jnp.exp2((m - m_new) * (scale * LOG2E))
    return m_new, l * a + part, acc * a + o


def hist_kernel(scale, n_whole, n_state, q_ref, *refs):
    state, kv, outs = refs[:n_state], refs[n_state:-3], refs[-3:]
    pairs = [(r, 0, r, r.shape[0] // 2) for r in kv[:n_whole]]
    pairs += [(a, 0, b, 0) for a, b in zip(kv[n_whole::2], kv[n_whole + 1::2])]
    q = q_ref[...]
    m = l = acc = None
    if state:
        m, l, acc = state[0][:, :1], state[1][...], state[2][...]
    for kr, k0, vr, v0 in pairs:
        rows = vr.shape[0] - v0
        m, l, acc = block(q, kr[k0:k0 + rows, :], vr[v0:v0 + rows, :], m, l, acc, scale)
    m_ref, l_ref, o_ref = outs
    m_ref[...] = jnp.broadcast_to(m, m_ref.shape)
    l_ref[...] = l
    o_ref[...] = acc


def new_kernel(scale, idx_ref, q_ref, k_ref, v_ref, m_ref, l_ref, o_ref, out_ref):
    n = q_ref.shape[0]
    q = q_ref[...]
    m, l, acc = m_ref[:, :1], l_ref[...], o_ref[...]
    qpos = idx_ref[0] * n + lax.broadcasted_iota(jnp.int32, (n, CHUNK), 0)
    col = lax.broadcasted_iota(jnp.int32, (n, CHUNK), 1)
    for c in range(k_ref.shape[0] // CHUNK):
        at = slice(c * CHUNK, (c + 1) * CHUNK)
        m, l, acc = block(q, k_ref[at, :], v_ref[at, :], m, l, acc, scale, col + c * CHUNK <= qpos)
    out_ref[...] = (acc / jnp.sum(l, axis=-1, keepdims=True)).astype(out_ref.dtype)


def heads_of(q, dh, kvl):
    g = q.shape[1] // dh // kvl
    return g, pl.BlockSpec((q.shape[0], dh), lambda i, j: (0, i * g + j)), lambda a: pl.BlockSpec((a.shape[0], dh), lambda i, j: (0, i))


def cost(q, n_keys, dh, kvl):
    return pl.CostEstimate(
        flops=8 * q.size * n_keys, bytes_accessed=8 * n_keys * kvl * dh, transcendentals=q.size // dh * n_keys)


def hist_attention(q, state, whole, halves, dh, kvl):
    g, head, keys = heads_of(q, dh, kvl)
    stat = jax.ShapeDtypeStruct(q.shape, jnp.float32)
    return pl.pallas_call(
        functools.partial(hist_kernel, dh ** -0.5, len(whole), len(state)),
        grid=(kvl, g),
        in_specs=[head] * (1 + len(state)) + [keys(a) for a in whole + halves],
        out_specs=[head] * 3,
        out_shape=(stat, stat, stat),
        compiler_params=PARAMS2,
        cost_estimate=cost(q, sum(a.shape[0] for a in whole + halves) // 2, dh, kvl),
        name='hist_attention',
    )(q, *state, *whole, *halves)


def new_attention(idx, q, state, k_all, v_all, dh, kvl):
    g, head, keys = heads_of(q, dh, kvl)
    return pl.pallas_call(
        functools.partial(new_kernel, dh ** -0.5),
        grid=(kvl, g),
        in_specs=[pl.BlockSpec(memory_space=pltpu.SMEM), head, keys(k_all), keys(v_all), head, head, head],
        out_specs=head,
        out_shape=jax.ShapeDtypeStruct(q.shape, jnp.bfloat16),
        compiler_params=PARAMS2,
        cost_estimate=cost(q, k_all.shape[0], dh, kvl),
        name='new_attention',
    )(idx, q, k_all, v_all, *state)


def solution(mesh):
    sp = mesh.shape['sp']
    tp = mesh.shape['tp']
    row = ('dp', 'sp')
    kv_spec = P(None, row, 'tp', None)
    col = P(None, None, 'tp')
    rowsplit = P(None, 'tp', None)
    right = [(i, (i + 2) % sp) for i in range(sp)]
    left = [(i, (i - 2) % sp) for i in range(sp)]
    other = [(i, i ^ 1) for i in range(sp)]

    def to_neighbours(own):
        return lax.ppermute(own, 'sp', right), lax.ppermute(own, 'sp', left)

    def to_far(from_left, from_right):
        half = from_left.shape[0] // 2
        return lax.ppermute(from_left[:half], 'sp', right), lax.ppermute(from_right[half:], 'sp', left)

    def to_other(*blocks):
        return tuple(lax.ppermute(a, 'sp', other) for a in blocks)

    after = lax.optimization_barrier

    def body(x, pos, k_hist, v_hist, wq, wk, wv, wo, wg, wu, wd, g1, g2):
        n, d = x.shape
        layers, nh, kvl, dh = k_hist.shape
        part = n // tp
        idx = lax.axis_index('sp').astype(jnp.int32)
        cos, sin = rope_tables(pos, dh)
        xs = lax.dynamic_slice_in_dim(x, lax.axis_index('tp') * part, part, axis=0)
        own = [
            jnp.concatenate([k_hist[l].reshape(nh, kvl * dh), v_hist[l].reshape(nh, kvl * dh)], axis=0)
            for l in range(layers)
        ]
        near = to_neighbours(own[0])
        own_o = to_other(own[0])

        ks, vs = [], []
        for l in range(layers):
            if l == 0:
                h, own_o = after((rmsnorm(x, g1[l]), own_o))
            else:
                h = lax.all_gather(rmsnorm(xs, g1[l]), 'tp', axis=0, tiled=True)
            q, k, v = qkv(h, wq, wk, wv, l, cos, sin)
            ks.append(k.reshape(n, kvl, dh))
            vs.append(v.reshape(n, kvl, dh))
            kv_all = lax.all_gather(jnp.stack([k, v]), 'sp', axis=1, tiled=True)
            if l == 0:
                state = hist_attention(q, (), [own[l], *own_o], [], dh, kvl)
                near, state = after((near, tuple(state)))
                far = to_far(*near)
                near_o = to_other(*near)
                state = hist_attention(q, state, [*near, *near_o], [], dh, kvl)
                far, state = after((far, tuple(state)))
                far_o = to_other(*far)
                state = hist_attention(q, state, [], [*far, *far_o], dh, kvl)
            else:
                state = hist_attention(q, (), [own[l], *near, *own_o, *near_o], [*far, *far_o], dh, kvl)
            if l + 1 < layers:
                own[l + 1], _ = after((own[l + 1], far))
                near = to_neighbours(own[l + 1])
            attn = new_attention(idx.reshape(1), q, state, kv_all[0], kv_all[1], dh, kvl)
            if l + 1 < layers:
                attn, near = after((attn, near))
                far = to_far(*near)
            y = by_columns(down_kernel, attn, (wo,), l, 1024, jnp.float32, 'attn_out')
            y = lax.psum_scatter(y, 'tp', scatter_dimension=0, tiled=True)
            xs = xs + y.astype(jnp.bfloat16)

            h2 = lax.all_gather(rmsnorm(xs, g2[l]), 'tp', axis=0, tiled=True)
            if l + 1 < layers:
                h2, far = after((h2, far))
                own_o, near_o, far_o = to_other(own[l + 1]), to_other(*near), to_other(*far)
            u = by_columns(gate_kernel, h2, (wg, wu), l, 512, jnp.bfloat16, 'gate_up')
            if l + 1 < layers:
                u, own_o, near_o, far_o = after((u, own_o, near_o, far_o))
            y = by_columns(down_kernel, u, (wd,), l, 512, jnp.float32, 'down')
            y = lax.psum_scatter(y, 'tp', scatter_dimension=0, tiled=True)
            xs = xs + y.astype(jnp.bfloat16)
        x = lax.all_gather(xs, 'tp', axis=0, tiled=True)
        return x, jnp.stack(ks), jnp.stack(vs)

    in_specs = (P(row, None), P(row), kv_spec, kv_spec, col, col, col, rowsplit, col, col, rowsplit, P(), P())
    out_specs = (P(row, None), kv_spec, kv_spec)
    return jax.shard_map(body, mesh=mesh, in_specs=in_specs, out_specs=out_specs, check_vma=False)
```

time: 1310 us -> 689 us (0.53)
  blocking collectives: 387 us -> 0 us
  matrix products: 359 us -> 0 us
  Pallas kernels: 0 us -> 264 us
  other arithmetic: 115 us -> 17.4 us
  local copies, waits for them, and re-layouts: 89.6 us -> 39.7 us
  waiting for transfers between devices: 324 us -> 340 us
    psum x4 -> x0, blocking collectives: 387 us -> none  [the longest x2 198 us: body(): x = x + lax.psum(mm(attn, wo[l]), 'tp').astype(jnp.bfloat16)]
    dot_general x158 -> x0, matrix products: 359 us -> none  [the longest x14 158 us: mm(): return jnp.dot(a, b, preferred_element_type=jnp.float32)]
    pallas_call x0 -> x14, Pallas kernels: none -> 264 us  [the longest x6 109 us: by_columns(): pl.pallas_call(kernel, grid=(pl.cdiv(f, cols),), in_specs=[pl.BlockSpec((...]
    reduce_scatter x2 -> x4, waiting for transfers between devices: 123 us -> 215 us  [body(): y = lax.psum_scatter(y, 'tp', scatter_dimension=0, tiled=True)]
    pmax x2 -> x0, waiting for transfers between devices: 88.7 us -> none  [body(): m_g = lax.pmax(m_h, 'sp')]
    reduce_sum x72 -> x0, other arithmetic: 50.1 us -> none  [partial_attn(): return (m, jnp.sum(p, axis=-1), o)]
    mul x4 -> x0, other arithmetic: 24 us -> none  [the longest x2 22 us: body(): o_h.reshape(s_tot, kvl, g, dh) * sc[..., None]]
    unnamed x14 -> x10, waiting for transfers between devices: 16.7 us -> 0.54 us
  transfers between devices with their start and end apart: 12 -> 28, of which waited for: 10 -> 11; matrix products, arithmetic and copies ran while one was open for 10% -> 1% of each run, Pallas kernels for 0% -> 22%
where the time goes in v1:
time: 689 us; the launch traced here: 687 us
  waiting for transfers between devices  340 us (49%)
  Pallas kernels  264 us (38%)
  local copies, waits for them, and re-layouts  39.7 us (6%)
  other arithmetic  17.4 us (3%)
  between operations  14.7 us (2%)
  starting transfers between devices  11.6 us (2%)
    reduce_scatter x4, waiting for transfers between devices, body(): y = lax.psum_scatter(y, 'tp', scatter_dimension=0, tiled=True)  215 us
    pallas_call x6, Pallas kernels, by_columns(): pl.pallas_call(kernel, grid=(pl.cdiv(f, cols),), in_specs=[pl.BlockSpec((...  109 us
    pallas_call x4, Pallas kernels, hist_attention(): pl.pallas_call(functools.partial(hist_kernel, dh ** (-0.5), len(whole), l...  98.2 us
    all_gather x2, waiting for transfers between devices, body(): h2 = lax.all_gather(rmsnorm(xs, g2[l]), 'tp', axis=0, tiled=True)  48.5 us
    pallas_call x2, Pallas kernels, new_attention(): pl.pallas_call(functools.partial(new_kernel, dh ** (-0.5)), grid=(kvl, g)...  32.9 us
    all_gather x1, waiting for transfers between devices, body(): h = lax.all_gather(rmsnorm(xs, g1[l]), 'tp', axis=0, tiled=True)  32.1 us
    unnamed x84, local copies, waits for them, and re-layouts  30.1 us
    all_gather x1, waiting for transfers between devices, body(): x = lax.all_gather(xs, 'tp', axis=0, tiled=True)  29.8 us
  transfers between devices with their start and end apart: 28, of which 11 were waited for; matrix products, arithmetic and copies ran while one was open for 1% of the time, Pallas kernels for 22%

profile of v1, /device:TPU:100, one launch (start us, length us, event | category | flops | bytes accessed | tf_op | source)
XLA Modules:
  0.0 686.7 jit_solution(7126615726025235712)
XLA Ops:
  7.3 2.8 fusion.13
  10.2 1.5 fusion.14
  11.9 1.4 collective-permute-start.1
  17.7 11.6 %qkv.2 = (bf16[256,1280]{1,0:T(8,128)(2,1)S(1)}, bf16[256,256]{1,0:T(8,128)(2,1)S(1)}, bf16[256,256]{1,0:T(8,128)(2,1)S(1)}) custom-call(bf16[256,5120]{1,0:T(8,128)(2,1)S(1)} %fusion.2.h_ref, bf16[2,5120,1280]{2,1,0:T(8,128)(2,1)} %wq_ref.3, bf16[2,5120,256]{2,1,0:T(8,128)(2,1)} %wk_ref.3, bf16[2,5120,256]{2,1,0:T(8,128)(2,1)} %wv_ref.3, ...), custom_call_target="tpu_custom_call" | custom-call | flops 4697620480 | bytes 18350080 | tf_op jit(solution)/shard_map/qkv/pallas_call | solution.py:71
  31.8 1.2 copy-done.10
  33.0 1.1 copy-done.12
  34.1 12.2 %hist_attention.4 = (f32[256,1280]{1,0:T(8,128)S(1)}, f32[256,1280]{1,0:T(8,128)S(1)}, f32[256,1280]{1,0:T(8,128)}) custom-call(bf16[256,1280]{1,0:T(8,128)(2,1)S(1)} %copy-done.12, bf16[2048,256]{1,0:T(8,128)(2,1)S(1)} %bitcast_dynamic-update-slice_fusion.refs_0_, bf16[2048,256]{1,0:T(8,128)(2,1)S(1)} %copy-done.10), custom_call_target="tpu_custom_call" | custom-call | flops 5368709120 | bytes 4194304 | tf_op jit(solution)/shard_map/hist_attention/pallas_call | solution.py:171
  46.3 1.1 copy-done.28
  47.4 1.1 copy-done.29
  49.1 1.4 collective-permute-start.3
  51.3 1.6 collective-permute-done.6.refs_6_
  52.9 28.2 %hist_attention.5 = (f32[256,1280]{1,0:T(8,128)S(1)}, f32[256,1280]{1,0:T(8,128)}, f32[256,1280]{1,0:T(8,128)}) custom-call(bf16[256,1280]{1,0:T(8,128)(2,1)S(1)} %copy-done.13, f32[256,1280]{1,0:T(8,128)} %copy-done.28, f32[256,1280]{1,0:T(8,128)} %copy-done.29, f32[256,1280]{1,0:T(8,128)} %get-tuple-element.58.refs_2_, ...), custom_call_target="tpu_custom_call" | custom-call | flops 10737418240 | bytes 8388608 | tf_op jit(solution)/shard_map/hist_attention/pallas_call | solution.py:171
  82.7 1.5 collective-permute-start.9
  84.2 16.7 %hist_attention.6 = (f32[256,1280]{1,0:T(8,128)S(1)}, f32[256,1280]{1,0:T(8,128)S(1)}, f32[256,1280]{1,0:T(8,128)}) custom-call(bf16[256,1280]{1,0:T(8,128)(2,1)S(1)} %copy-done.13, f32[256,1280]{1,0:T(8,128)} %copy-done.27, f32[256,1280]{1,0:T(8,128)} %get-tuple-element.63.refs_1_, f32[256,1280]{1,0:T(8,128)} %get-tuple-element.64.refs_2_, ...), custom_call_target="tpu_custom_call" | custom-call | flops 5368709120 | bytes 4194304 | tf_op jit(solution)/shard_map/hist_attention/pallas_call | solution.py:171
  103.1 1.8 slice_bitcast_fusion.2
  105.6 16.5 %new_attention.2.u_ref = bf16[256,1280]{1,0:T(8,128)(2,1)S(1)} custom-call(s32[1]{0:T(128)} %bitcast.idx_ref, bf16[256,1280]{1,0:T(8,128)(2,1)S(1)} %copy-done.14, bf16[2048,256]{1,0:T(8,128)(2,1)S(1)} %get-tuple-element.98.k_ref, bf16[2048,256]{1,0:T(8,128)(2,1)S(1)} %get-tuple-element.97.v_ref, f32[256,1280]{1,0:T(8,128)S(1)} %copy-done.24, ...), custom_call_target="tpu_custom_call" | custom-call | flops 5368709120 | bytes 4194304 | tf_op jit(solution)/shard_map/new_attention/pallas_call | solution.py:185
  122.1 8.0 %attn_out.2 = f32[256,5120]{1,0:T(8,128)S(1)} custom-call(bf16[256,1280]{1,0:T(8,128)(2,1)S(1)} %new_attention.2.u_ref, bf16[2,1280,5120]{2,1,0:T(8,128)(2,1)} %w_ref.6), custom_call_target="tpu_custom_call" | custom-call | flops 3355443200 | bytes 13107200 | tf_op jit(solution)/shard_map/attn_out/pallas_call | solution.py:98
  130.1 2.3 copy-done
  133.8 55.7 %reduce-scatter.5.cloned.1.call-done = f32[64,5120]{1,0:T(8,128)} async-done(((f32[256,5120]{1,0:T(8,128)}), f32[64,5120]{1,0:T(8,128)}) %reduce-scatter.5.cloned.1.call-update) | async-done | bytes 1310736 | tf_op jit(solution)/shard_map/reduce_scatter | solution.py:263
  189.5 1.8 fusion.3
  193.6 1.3 collective-permute-start.11
  196.3 10.8 %collective-permute-done.11.refs_6_ = bf16[1024,256]{1,0:T(8,128)(2,1)S(1)} collective-permute-done((bf16[1024,256]{1,0:T(8,128)(2,1)S(1)}, bf16[1024,256]{1,0:T(8,128)(2,1)S(1)}, u32[]{:S(2)}, u32[]{:S(2)}) %collective-permute-start.11) | collective-permute-done | bytes 524320 | tf_op jit(solution)/shard_map/ppermute | solution.py:213
  208.1 16.5 %all-gather.9.cloned.1.call-done.h_ref = bf16[256,5120]{1,0:T(8,128)(2,1)} async-done(((bf16[64,5120]{1,0:T(8,128)(2,1)}), bf16[256,5120]{1,0:T(8,128)(2,1)}) %all-gather.9.cloned.1.call-update) | async-done | bytes 2621456 | tf_op jit(solution)/shard_map/all_gather | solution.py:266
  225.1 1.7 copy-done.3
  226.8 27.4 %gate_up.2.u_ref = bf16[256,3456]{1,0:T(8,128)(2,1)S(1)} custom-call(bf16[256,5120]{1,0:T(8,128)(2,1)S(1)} %copy-done.3, bf16[2,5120,3456]{2,1,0:T(8,128)(2,1)} %wg_ref.3, bf16[2,5120,3456]{2,1,0:T(8,128)(2,1)} %wu_ref.3), custom_call_target="tpu_custom_call" | custom-call | flops 18119393280 | bytes 70778880 | tf_op jit(solution)/shard_map/gate_up/pallas_call | solution.py:98
  255.8 19.2 %down.2 = f32[256,5120]{1,0:T(8,128)} custom-call(bf16[256,3456]{1,0:T(8,128)(2,1)S(1)} %gate_up.2.u_ref, bf16[2,3456,5120]{2,1,0:T(8,128)(2,1)} %w_ref.7), custom_call_target="tpu_custom_call" | custom-call | flops 9059696640 | bytes 35389440 | tf_op jit(solution)/shard_map/down/pallas_call | solution.py:98
  275.2 53.2 %reduce-scatter.7.cloned.1.call-done = f32[64,5120]{1,0:T(8,128)} async-done(((f32[256,5120]{1,0:T(8,128)}), f32[64,5120]{1,0:T(8,128)}) %reduce-scatter.7.cloned.1.call-update) | async-done | bytes 1310736 | tf_op jit(solution)/shard_map/reduce_scatter | solution.py:274
  328.4 1.6 fusion.6
  332.1 32.1 %all-gather.11.cloned.1.call-done.h_ref = bf16[256,5120]{1,0:T(8,128)(2,1)} async-done(((bf16[64,5120]{1,0:T(8,128)(2,1)}), bf16[256,5120]{1,0:T(8,128)(2,1)}) %all-gather.11.cloned.1.call-update) | async-done | bytes 2621456 | tf_op jit(solution)/shard_map/all_gather | solution.py:239
  364.1 1.7 copy-done.2
  365.9 11.6 %qkv.3 = (bf16[256,1280]{1,0:T(8,128)(2,1)S(1)}, bf16[256,256]{1,0:T(8,128)(2,1)S(1)}, bf16[256,256]{1,0:T(8,128)(2,1)S(1)}) custom-call(bf16[256,5120]{1,0:T(8,128)(2,1)S(1)} %copy-done.2, bf16[2,5120,1280]{2,1,0:T(8,128)(2,1)} %wq_ref.3, bf16[2,5120,256]{2,1,0:T(8,128)(2,1)} %wk_ref.3, bf16[2,5120,256]{2,1,0:T(8,128)(2,1)} %wv_ref.3, ...), custom_call_target="tpu_custom_call" | custom-call | flops 4697620480 | bytes 18350080 | tf_op jit(solution)/shard_map/qkv/pallas_call | solution.py:71
  381.7 41.1 %hist_attention.7 = (f32[256,1280]{1,0:T(8,128)}, f32[256,1280]{1,0:T(8,128)}, f32[256,1280]{1,0:T(8,128)}) custom-call(bf16[256,1280]{1,0:T(8,128)(2,1)S(1)} %get-tuple-element.78.q_ref, bf16[2048,256]{1,0:T(8,128)(2,1)S(1)} %pad_maximum_fusion.refs_0_, bf16[2048,256]{1,0:T(8,128)(2,1)} %collective-permute-done.9.refs_1_, ...), custom_call_target="tpu_custom_call" | custom-call | flops 21474836480 | bytes 16777216 | tf_op jit(solution)/shard_map/hist_attention/pallas_call | solution.py:171
  422.8 1.8 slice_bitcast_fusion
  425.1 16.5 %new_attention.3.u_ref = bf16[256,1280]{1,0:T(8,128)(2,1)S(1)} custom-call(s32[1]{0:T(128)} %bitcast.idx_ref, bf16[256,1280]{1,0:T(8,128)(2,1)S(1)} %get-tuple-element.78.q_ref, bf16[2048,256]{1,0:T(8,128)(2,1)S(1)} %get-tuple-element.96.k_ref, bf16[2048,256]{1,0:T(8,128)(2,1)S(1)} %get-tuple-element.95.v_ref, f32[256,1280]{1,0:T(8,128)S(1)} %copy-done.21, ...), custom_call_target="tpu_custom_call" | custom-call | flops 5368709120 | bytes 4194304 | tf_op jit(solution)/shard_map/new_attention/pallas_call | solution.py:185
  441.5 8.0 %attn_out.3 = f32[256,5120]{1,0:T(8,128)S(1)} custom-call(bf16[256,1280]{1,0:T(8,128)(2,1)S(1)} %new_attention.3.u_ref, bf16[2,1280,5120]{2,1,0:T(8,128)(2,1)} %w_ref.6), custom_call_target="tpu_custom_call" | custom-call | flops 3355443200 | bytes 13107200 | tf_op jit(solution)/shard_map/attn_out/pallas_call | solution.py:98
  449.6 2.3 copy-done.1
  452.1 53.2 %reduce-scatter.9.cloned.1.call-done = f32[64,5120]{1,0:T(8,128)} async-done(((f32[256,5120]{1,0:T(8,128)}), f32[64,5120]{1,0:T(8,128)}) %reduce-scatter.9.cloned.1.call-update) | async-done | bytes 1310736 | tf_op jit(solution)/shard_map/reduce_scatter | solution.py:263
  505.3 1.6 fusion.9
  508.1 32.1 %all-gather.15.cloned.1.call-done.h_ref = bf16[256,5120]{1,0:T(8,128)(2,1)} async-done(((bf16[64,5120]{1,0:T(8,128)(2,1)}), bf16[256,5120]{1,0:T(8,128)(2,1)}) %all-gather.15.cloned.1.call-update) | async-done | bytes 2621456 | tf_op jit(solution)/shard_map/all_gather | solution.py:266
  540.2 1.7 copy-done.4
  541.9 27.5 %gate_up.3.u_ref = bf16[256,3456]{1,0:T(8,128)(2,1)S(1)} custom-call(bf16[256,5120]{1,0:T(8,128)(2,1)S(1)} %copy-done.4, bf16[2,5120,3456]{2,1,0:T(8,128)(2,1)} %wg_ref.3, bf16[2,5120,3456]{2,1,0:T(8,128)(2,1)} %wu_ref.3), custom_call_target="tpu_custom_call" | custom-call | flops 18119393280 | bytes 70778880 | tf_op jit(solution)/shard_map/gate_up/pallas_call | solution.py:98
  569.4 19.3 %down.3 = f32[256,5120]{1,0:T(8,128)} custom-call(bf16[256,3456]{1,0:T(8,128)(2,1)S(1)} %gate_up.3.u_ref, bf16[2,3456,5120]{2,1,0:T(8,128)(2,1)} %w_ref.7), custom_call_target="tpu_custom_call" | custom-call | flops 9059696640 | bytes 35389440 | tf_op jit(solution)/shard_map/down/pallas_call | solution.py:98
  588.8 53.2 %reduce-scatter.11.cloned.1.call-done = f32[64,5120]{1,0:T(8,128)} async-done(((f32[256,5120]{1,0:T(8,128)}), f32[64,5120]{1,0:T(8,128)}) %reduce-scatter.11.cloned.1.call-update) | async-done | bytes 1310736 | tf_op jit(solution)/shard_map/reduce_scatter | solution.py:274
  642.0 2.2 convert_add_fusion
  644.5 1.1 pad_maximum_fusion.3
  645.5 1.1 pad_maximum_fusion.4
  646.6 29.8 %all-gather.17.cloned.1.call-done = bf16[256,5120]{1,0:T(8,128)(2,1)} async-done(((bf16[64,5120]{1,0:T(8,128)(2,1)}), bf16[256,5120]{1,0:T(8,128)(2,1)}) %all-gather.17.cloned.1.call-update) | async-done | bytes 2621456 | tf_op jit(solution)/shard_map/all_gather | solution.py:276
  676.4 3.4 copy.26
  (154 shorter events, 29.4 us)
Async XLA Ops:
  7.2 3.0 copy-start.35
  7.2 95.9 %all-gather.7.cloned.1.call-start = ((), (), s32[]{:S(2)}) async-start(), calls=%async_computation.4 | async-start | bytes 2359296 | tf_op jit(solution)/shard_map/all_gather | solution.py:243
  10.2 3.9 copy-start.40
  10.2 3.9 copy-start.36
  10.2 4.5 copy-start.30
  11.8 5.0 collective-permute-start
  11.9 36.6 %collective-permute-start.1 = (bf16[2048,256]{1,0:T(8,128)(2,1)S(1)}, bf16[2048,256]{1,0:T(8,128)(2,1)S(1)}, u32[]{:S(2)}, u32[]{:S(2)}) collective-permute-start(bf16[2048,256]{1,0:T(8,128)(2,1)S(1)} %bitcast_dynamic-update-slice_fusion.refs_0_), channel_id=1, source_target_pairs={{0,2},{1,3},{2,4},{3,5},{4,6},{5,7},{6,0},{7,1},{8,10},{9,11},{10,... | collective-permute-start | bytes 3145736 | tf_op jit(solution)/shard_map/ppermute | solution.py:209
  13.3 35.2 %collective-permute-start.2 = (bf16[2048,256]{1,0:T(8,128)(2,1)S(1)}, bf16[2048,256]{1,0:T(8,128)(2,1)S(1)}, u32[]{:S(2)}, u32[]{:S(2)}) collective-permute-start(bf16[2048,256]{1,0:T(8,128)(2,1)S(1)} %bitcast_dynamic-update-slice_fusion.refs_0_), channel_id=1, source_target_pairs={{0,6},{1,7},{2,0},{3,1},{4,2},{5,3},{6,4},{7,5},{8,14},{9,15},{10,... | collective-permute-start | bytes 3145736 | tf_op jit(solution)/shard_map/ppermute | solution.py:209
  31.7 157.8 %reduce-scatter.5.cloned.1.call-start = ((), (), s32[]{:S(2)}) async-start(), calls=%async_computation.5 | async-start | bytes 6553600 | tf_op jit(solution)/shard_map/reduce_scatter | solution.py:263
  48.5 2.8 collective-permute-start.5
  48.6 4.4 collective-permute-start.6
  49.0 3.9 copy-start.13
  49.1 32.6 %copy-start.33 = (bf16[1,1024,2,128]{3,2,1,0:T(2,128)(2,1)S(1)}, bf16[1,1024,2,128]{3,2,1,0:T(2,128)(2,1)}, u32[]{:S(2)}) copy-start(bf16[1,1024,2,128]{3,2,1,0:T(2,128)(2,1)} %get-tuple-element.99) | copy-start | bytes 1572868
  49.1 32.6 %copy-start.34 = (bf16[1,1024,2,128]{3,2,1,0:T(2,128)(2,1)S(1)}, bf16[1,1024,2,128]{3,2,1,0:T(2,128)(2,1)}, u32[]{:S(2)}) copy-start(bf16[1,1024,2,128]{3,2,1,0:T(2,128)(2,1)} %get-tuple-element.101) | copy-start | bytes 1572868
  49.1 32.0 %collective-permute-start.3 = (bf16[1024,256]{1,0:T(8,128)(2,1)S(1)}, bf16[1024,256]{1,0:T(8,128)(2,1)S(1)}, u32[]{:S(2)}, u32[]{:S(2)}) collective-permute-start(bf16[1024,256]{1,0:T(8,128)(2,1)S(1)} %slice.53), channel_id=1, source_target_pairs={{0,2},{1,3},{2,4},{3,5},{4,6},{5,7},{6,0},{7,1},{8,10},{9,11},{10,... | collective-permute-start | bytes 1572872 | tf_op jit(solution)/shard_map/ppermute | solution.py:213
  50.6 30.6 %collective-permute-start.4 = (bf16[1024,256]{1,0:T(8,128)(2,1)S(1)}, bf16[1024,256]{1,0:T(8,128)(2,1)S(1)}, u32[]{:S(2)}, u32[]{:S(2)}) collective-permute-start(bf16[1024,256]{1,0:T(8,128)(2,1)S(1)} %slice.54), channel_id=1, source_target_pairs={{0,6},{1,7},{2,0},{3,1},{4,2},{5,3},{6,4},{7,5},{8,14},{9,15},{10,... | collective-permute-start | bytes 1572872 | tf_op jit(solution)/shard_map/ppermute | solution.py:213
  81.2 3.1 collective-permute-start.7
  81.4 2.8 collective-permute-start.8
  82.2 39.9 %collective-permute-start.10 = (bf16[2048,256]{1,0:T(8,128)(2,1)S(1)}, bf16[2048,256]{1,0:T(8,128)(2,1)S(1)}, u32[]{:S(2)}, u32[]{:S(2)}) collective-permute-start(bf16[2048,256]{1,0:T(8,128)(2,1)S(1)} %pad_maximum_fusion.refs_0_), channel_id=1, source_target_pairs={{0,6},{1,7},{2,0},{3,1},{4,2},{5,3},{6,4},{7,5},{8,14},{9,15},{10,... | collective-permute-start | bytes 3145736 | tf_op jit(solution)/shard_map/ppermute | solution.py:209
  82.7 39.4 %collective-permute-start.9 = (bf16[2048,256]{1,0:T(8,128)(2,1)S(1)}, bf16[2048,256]{1,0:T(8,128)(2,1)}, u32[]{:S(2)}, u32[]{:S(2)}) collective-permute-start(bf16[2048,256]{1,0:T(8,128)(2,1)S(1)} %pad_maximum_fusion.refs_0_), channel_id=1, source_target_pairs={{0,2},{1,3},{2,4},{3,5},{4,6},{5,7},{6,0},{7,1},{8,10},{9,11},{10,... | collective-permute-start | bytes 3145736 | tf_op jit(solution)/shard_map/ppermute | solution.py:209
  103.1 1.8 copy-start.14
  103.1 2.1 copy-start.24
  103.1 2.5 copy-start.26
  130.1 2.4 copy-start
  132.5 92.0 %all-gather.9.cloned.1.call-start = ((), (), s32[]{:S(2)}) async-start(), calls=%async_computation.6 | async-start | bytes 3276800 | tf_op jit(solution)/shard_map/all_gather | solution.py:266
  192.4 136.0 %reduce-scatter.7.cloned.1.call-start = ((), (), s32[]{:S(2)}) async-start(), calls=%async_computation.7 | async-start | bytes 6553600 | tf_op jit(solution)/shard_map/reduce_scatter | solution.py:274
  193.6 13.5 %collective-permute-start.11 = (bf16[1024,256]{1,0:T(8,128)(2,1)S(1)}, bf16[1024,256]{1,0:T(8,128)(2,1)S(1)}, u32[]{:S(2)}, u32[]{:S(2)}) collective-permute-start(bf16[1024,256]{1,0:T(8,128)(2,1)S(1)} %slice.58), channel_id=1, source_target_pairs={{0,2},{1,3},{2,4},{3,5},{4,6},{5,7},{6,0},{7,1},{8,10},{9,11},{10,... | collective-permute-start | bytes 1572872 | tf_op jit(solution)/shard_map/ppermute | solution.py:213
  194.9 13.2 %collective-permute-start.12 = (bf16[1024,256]{1,0:T(8,128)(2,1)S(1)}, bf16[1024,256]{1,0:T(8,128)(2,1)}, u32[]{:S(2)}, u32[]{:S(2)}) collective-permute-start(bf16[1024,256]{1,0:T(8,128)(2,1)S(1)} %slice.59), channel_id=1, source_target_pairs={{0,6},{1,7},{2,0},{3,1},{4,2},{5,3},{6,4},{7,5},{8,14},{9,15},{10,... | collective-permute-start | bytes 1572872 | tf_op jit(solution)/shard_map/ppermute | solution.py:213
  195.8 58.4 %collective-permute-start.13 = (bf16[2048,256]{1,0:T(8,128)(2,1)S(1)}, bf16[2048,256]{1,0:T(8,128)(2,1)}, u32[]{:S(2)}, u32[]{:S(2)}) collective-permute-start(bf16[2048,256]{1,0:T(8,128)(2,1)S(1)} %pad_maximum_fusion.refs_0_), channel_id=1, source_target_pairs={{0,1},{1,0},{2,3},{3,2},{4,5},{5,4},{6,7},{7,6},{8,9},{9,8},{10,11... | collective-permute-start | bytes 3145736 | tf_op jit(solution)/shard_map/ppermute | solution.py:216
  195.8 58.4 %collective-permute-start.14 = (bf16[2048,256]{1,0:T(8,128)(2,1)}, bf16[2048,256]{1,0:T(8,128)(2,1)}, u32[]{:S(2)}, u32[]{:S(2)}) collective-permute-start(bf16[2048,256]{1,0:T(8,128)(2,1)} %collective-permute-done.9.refs_1_), channel_id=1, source_target_pairs={{0,1},{1,0},{2,3},{3,2},{4,5},{5,4},{6,7},{7,6},{8,9},{9,8},{10,11... | collective-permute-start | bytes 3145736 | tf_op jit(solution)/shard_map/ppermute | solution.py:216
  196.3 57.9 %collective-permute-start.15 = (bf16[2048,256]{1,0:T(8,128)(2,1)S(1)}, bf16[2048,256]{1,0:T(8,128)(2,1)}, u32[]{:S(2)}, u32[]{:S(2)}) collective-permute-start(bf16[2048,256]{1,0:T(8,128)(2,1)S(1)} %collective-permute-done.10.refs_2_), channel_id=1, source_target_pairs={{0,1},{1,0},{2,3},{3,2},{4,5},{5,4},{6,7},{7,6},{8,9},{9,8},{10,11... | collective-permute-start | bytes 3145736 | tf_op jit(solution)/shard_map/ppermute | solution.py:216
  207.1 47.1 %copy-start.15 = (bf16[1024,256]{1,0:T(8,128)(2,1)}, bf16[1024,256]{1,0:T(8,128)(2,1)S(1)}, u32[]{:S(2)}) copy-start(bf16[1024,256]{1,0:T(8,128)(2,1)S(1)} %collective-permute-done.11.refs_6_) | copy-start | bytes 1572868
  224.6 29.7 %collective-permute-start.16 = (bf16[1024,256]{1,0:T(8,128)(2,1)S(1)}, bf16[1024,256]{1,0:T(8,128)(2,1)S(1)}, u32[]{:S(2)}, u32[]{:S(2)}) collective-permute-start(bf16[1024,256]{1,0:T(8,128)(2,1)S(1)} %collective-permute-done.11.refs_6_), channel_id=1, source_target_pairs={{0,1},{1,0},{2,3},{3,2},{4,5},{5,4},{6,7},{7,6},{8,9},{9,8},{10,11... | collective-permute-start | bytes 1572872 | tf_op jit(solution)/shard_map/ppermute | solution.py:216
  224.6 30.5 %collective-permute-start.17 = (bf16[1024,256]{1,0:T(8,128)(2,1)}, bf16[1024,256]{1,0:T(8,128)(2,1)S(1)}, u32[]{:S(2)}, u32[]{:S(2)}) collective-permute-start(bf16[1024,256]{1,0:T(8,128)(2,1)} %collective-permute-done.12.refs_7_), channel_id=1, source_target_pairs={{0,1},{1,0},{2,3},{3,2},{4,5},{5,4},{6,7},{7,6},{8,9},{9,8},{10,11... | collective-permute-start | bytes 1572872 | tf_op jit(solution)/shard_map/ppermute | solution.py:216
  275.2 55.7 %copy-start.38 = (f32[1,5120]{1,0:T(1,128)S(1)}, f32[1,5120]{1,0:T(1,128)}, u32[]{:S(2)}) copy-start(f32[1,5120]{1,0:T(1,128)} %get-tuple-element.105) | copy-start | bytes 61444
  275.2 89.0 %all-gather.11.cloned.1.call-start = ((), (), s32[]{:S(2)}) async-start(), calls=%async_computation.8 | async-start | bytes 3276800 | tf_op jit(solution)/shard_map/all_gather | solution.py:239
  332.0 90.7 %all-gather.13.cloned.1.call-start = ((), (), s32[]{:S(2)}) async-start(), calls=%async_computation.9 | async-start | bytes 2359296 | tf_op jit(solution)/shard_map/all_gather | solution.py:243
  378.2 127.1 %reduce-scatter.9.cloned.1.call-start = ((), (), s32[]{:S(2)}) async-start(), calls=%async_computation.10 | async-start | bytes 6553600 | tf_op jit(solution)/shard_map/reduce_scatter | solution.py:263
  422.7 1.9 copy-start.21
  422.7 2.3 copy-start.22
  449.6 2.4 copy-start.1
  451.9 53.4 %copy-start.32 = (bf16[64,5120]{1,0:T(8,128)(2,1)S(1)}, bf16[64,5120]{1,0:T(8,128)(2,1)}, u32[]{:S(2)}) copy-start(bf16[64,5120]{1,0:T(8,128)(2,1)} %copy-done.31) | copy-start | bytes 1966084
  452.0 54.9 %copy-start.39 = (f32[1,5120]{1,0:T(1,128)S(1)}, f32[1,5120]{1,0:T(1,128)}, u32[]{:S(2)}) copy-start(f32[1,5120]{1,0:T(1,128)} %get-tuple-element.103) | copy-start | bytes 61444
  452.0 88.2 %all-gather.15.cloned.1.call-start = ((), (), s32[]{:S(2)}) async-start(), calls=%async_computation.11 | async-start | bytes 3276800 | tf_op jit(solution)/shard_map/all_gather | solution.py:266
  508.1 133.9 %reduce-scatter.11.cloned.1.call-start = ((), (), s32[]{:S(2)}) async-start(), calls=%async_computation.12 | async-start | bytes 6553600 | tf_op jit(solution)/shard_map/reduce_scatter | solution.py:274
  588.7 55.6 %copy-start.8 = (bf16[256,256]{1,0:T(8,128)(2,1)S(1)}, bf16[256,256]{1,0:T(8,128)(2,1)}, u32[]{:S(2)}) copy-start(bf16[256,256]{1,0:T(8,128)(2,1)} %copy-done.7) | copy-start | bytes 393220
  588.7 55.6 %copy-start.6 = (bf16[256,256]{1,0:T(8,128)(2,1)S(1)}, bf16[256,256]{1,0:T(8,128)(2,1)}, u32[]{:S(2)}) copy-start(bf16[256,256]{1,0:T(8,128)(2,1)} %copy-done.5) | copy-start | bytes 393220
  588.8 87.7 %all-gather.17.cloned.1.call-start = ((), (), s32[]{:S(2)}) async-start(), calls=%async_computation.13 | async-start | bytes 3276800 | tf_op jit(solution)/shard_map/all_gather | solution.py:276
  (21 other events, 22.4 us)
Sparse Core Ops, SparseCore 0:
  31.8 25.5 all-gather.6
  132.7 56.8 reduce-scatter.4
  192.6 31.9 all-gather.8
  275.3 53.0 reduce-scatter.6
  332.1 31.9 all-gather.10
  378.4 21.8 all-gather.12
  452.1 53.1 reduce-scatter.8
  508.2 31.9 all-gather.14
  588.9 53.0 reduce-scatter.10
  644.4 31.9 all-gather.16
